TPU v7x, 32 devices: a whole 2x2x4 slice. The times are simulated.
32 devices in a mesh: grid: 8 (over y, x, core), band: 4 (over z).
Axes of the slice: x: 2, y: 2, z: 4, core: 2. Of those that a mesh axis runs over, the one named last changes fastest.
Arguments:
- orbitals: bfloat16 [32, 64, 64, 128], P('band', 'grid'), may hold values from -6 to 6
- occupation: int32 [32], P('band'), may hold values from 1 to 2
- spin_of_band: int32 [32], P('band'), may hold values from 0 to 1
- ionic_charge: float32 [64, 64, 128], P('grid'), may hold values from 0.3 to 3
Outputs:
- potential: float32 [2, 64, 64, 128], P(None, 'grid')
- applied: bfloat16 [32, 64, 64, 128], P('band', 'grid')
All inputs are finite; a program needn't handle non-finite values.
Results may differ from a plain program's by a relative error of at most 0.001.
Values sent between devices are 32-bit elements; how exact they have to be, the bound alone decides.
A program may use at most 64 MiB of HBM per device.

v0:
```python
import math
import jax
import jax.numpy as jnp
from jax import lax
from jax.sharding import PartitionSpec as P

NZ = 64
spacing = 0.25
highest = lax.Precision.HIGHEST


def tables(count):
    index = jnp.arange(count, dtype=jnp.int32)
    product = index[:, None] * index[None, :] % count
    angle = 2.0 * math.pi * product.astype(jnp.float32) / count
    return (jnp.cos(angle), jnp.sin(angle))


def signed_sq(index, count):
    signed = jnp.where(index < count // 2, index, index - count).astype(jnp.float32)
    wave = 2.0 * math.pi * signed / (count * spacing)
    return wave * wave


def kernel_at(depth, row_index, rows, col_index, cols):
    g_sq = signed_sq(jnp.arange(depth, dtype=jnp.int32), depth)[:, None, None]
    g_sq = g_sq + signed_sq(row_index, rows)[None, :, None]
    g_sq = g_sq + signed_sq(col_index, cols)[None, None, :]
    return jnp.where(g_sq > 0, 4.0 * math.pi / jnp.where(g_sq > 0, g_sq, 1.0), 0.0)


def along(table, field, form):
    return jnp.einsum(form, table, field, precision=highest)


def forward_y(cos_y, sin_y, real_x, imag_x):
    form_y = "ky,zyx->zkx"
    real_y = along(cos_y, real_x, form_y) + along(sin_y, imag_x, form_y)
    imag_y = along(cos_y, imag_x, form_y) - along(sin_y, real_x, form_y)
    return (real_y, imag_y)


def inverse_y(cos_y, sin_y, real_k, imag_k):
    form_y = "ky,zyx->zkx"
    plane_real = along(cos_y, real_k, form_y) - along(sin_y, imag_k, form_y)
    plane_imag = along(cos_y, imag_k, form_y) + along(sin_y, real_k, form_y)
    return (plane_real, plane_imag)


def z_kernel(cos_z, sin_z, moved, kernel):
    form_z = "kz,zyx->kyx"
    real_z = along(cos_z, moved[0], form_z) + along(sin_z, moved[1], form_z)
    imag_z = along(cos_z, moved[1], form_z) - along(sin_z, moved[0], form_z)
    real_k = real_z * kernel
    imag_k = imag_z * kernel
    back_real = along(cos_z, real_k, form_z) - along(sin_z, imag_k, form_z)
    back_imag = along(cos_z, imag_k, form_z) + along(sin_z, real_k, form_z)
    return jnp.stack([back_real, back_imag])


def solve_hartree(net, depth):
    planes, rows, cols = net.shape
    cos_x, sin_x = tables(cols)
    cos_y, sin_y = tables(rows)
    cos_z, sin_z = tables(depth)
    local_rows = rows // lax.axis_size("grid")
    row_index = lax.axis_index("grid") * local_rows + jnp.arange(local_rows, dtype=jnp.int32)
    real_x = jnp.dot(net, cos_x, precision=highest)
    imag_x = -jnp.dot(net, sin_x, precision=highest)
    real_y, imag_y = forward_y(cos_y, sin_y, real_x, imag_x)
    moved = lax.all_to_all(
        jnp.stack([real_y, imag_y]), "grid", split_axis=2, concat_axis=1, tiled=True
    )
    kernel = kernel_at(depth, row_index, rows, jnp.arange(cols, dtype=jnp.int32), cols)
    back = z_kernel(cos_z, sin_z, moved, kernel)
    returned = lax.all_to_all(back, "grid", split_axis=1, concat_axis=2, tiled=True)
    plane_real, plane_imag = inverse_y(cos_y, sin_y, returned[0], returned[1])
    result = jnp.dot(plane_real, cos_x, precision=highest) - jnp.dot(
        plane_imag, sin_x, precision=highest
    )
    return result / (cols * rows * depth)


def local(orbitals, occupation, spin_of_band, ionic_charge):
    bands, planes, rows, cols = orbitals.shape
    total = bands * lax.axis_size("band")
    channels = jnp.arange(2, dtype=jnp.int32)
    weights = (
        jnp.where(
            spin_of_band[None, :] == channels[:, None], occupation[None, :].astype(jnp.float32), 0.0
        )
        / total
    )
    values = orbitals.astype(jnp.float32)
    squares = (values * values).reshape(bands, -1)
    partial_value = jnp.dot(weights, squares, precision=highest).reshape(2, planes, rows, cols)
    share = lax.psum_scatter(partial_value, "band", scatter_dimension=2, tiled=True)
    share_rows = share.shape[2]
    ion_share = lax.dynamic_slice_in_dim(
        ionic_charge, lax.axis_index("band") * share_rows, share_rows, 1
    )
    fields = jnp.concatenate(
        [-jnp.cbrt(6.0 / math.pi * share), (share[0] + share[1] - ion_share)[None]], 0
    )
    whole = lax.all_gather(fields, "band", axis=2, tiled=True)
    potential = solve_hartree(whole[2], NZ)[None] + whole[:2]
    pick = (spin_of_band[:, None] == channels[None, :]).astype(jnp.float32)
    chosen = jnp.dot(pick, potential.reshape(2, -1), precision=highest).reshape(
        bands, planes, rows, cols
    )
    applied = (chosen * values).astype(jnp.bfloat16)
    return (potential, applied)


def solution(mesh):
    return jax.shard_map(
        local,
        mesh=mesh,
        in_specs=(P("band", "grid", None, None), P("band"), P("band"), P("grid", None, None)),
        out_specs=(P(None, "grid", None, None), P("band", "grid", None, None)),
        check_vma=False,
    )
```

profile of v0, /device:TPU:0, one launch (start us, length us, event | category | flops | bytes accessed | tf_op | source)
XLA Modules:
  0.0 105.7 jit_solution(1825945070237419519)
XLA Ops:
  7.2 0.0 reduce-scatter.2.cloned.1.call-start
  7.2 0.7 convert_element_type.76
  7.9 3.5 %fusion.1 = f32[2,8,64,128]{3,0,2,1:T(2,128)S(1)} fusion(bf16[8,8,64,128]{3,2,1,0:T(8,128)(2,1)} %param.4, f32[8]{0:T(128)S(1)} %convert_element_type.76, s32[8]{0:T(128)} %param.6), kind=kOutput, calls=%fused_computation.3 | convolution fusion | flops 13631536 | bytes 1572928 | tf_op jit(solution)/shard_map/dot_general | solution.py:96
  11.3 1.1 %copy.29 = f32[2,8,64,128]{3,1,0,2:T(8,128)} copy(f32[2,8,64,128]{3,0,2,1:T(2,128)S(1)} %fusion.1) | data formatting | bytes 1048576 | tf_op jit(solution)/shard_map/dot_general | solution.py:96
  12.4 0.0 reduce-scatter.2.cloned.1.call-update
  12.5 24.7 %reduce-scatter.2.cloned.1.call-done = f32[2,8,16,128]{3,1,0,2:T(8,128)} async-done(((f32[2,8,64,128]{3,1,0,2:T(8,128)}), f32[2,8,16,128]{3,1,0,2:T(8,128)}) %reduce-scatter.2.cloned.1.call-update) | async-done | bytes 131088 | tf_op jit(solution)/shard_map/reduce_scatter | solution.py:97
  37.2 1.0 cbrt_negate_fusion
  38.2 0.9 fusion.34
  39.1 17.2 %all_gather.3 = f32[3,8,64,128]{3,2,1,0:T(8,128)S(1)} all-gather(f32[3,8,16,128]{3,2,1,0:T(8,128)S(1)} %pad_maximum_fusion.2), channel_id=1, replica_groups=mesh['grid'=8,'band'=4] {'band'}, dimensions={2}, use_global_device_ids=true | all-gather | bytes 983040 | tf_op jit(solution)/shard_map/all_gather | solution.py:105
  56.3 0.6 convolution_negate_fusion
  57.0 0.6 fusion.22
  57.6 0.5 fusion.64
  58.1 0.5 fusion.62
  58.6 0.5 fusion.12
  59.2 0.5 fusion.11
  59.8 1.1 %copy.33 = f32[2,8,64,128]{3,1,0,2:T(8,128)} copy(f32[2,8,64,128]{3,2,1,0:T(8,128)S(1)} %pad_maximum_fusion) | data formatting | bytes 1048576 | tf_op jit(solution)/shard_map/stack | solution.py:72
  60.9 3.6 %all-to-all-start = ((f32[2,8,64,128]{3,1,0,2:T(8,128)}), f32[2,8,64,128]{3,1,0,2:T(8,128)S(1)}, u32[]{:S(2)}, u32[]{:S(2)}) async-start(f32[2,8,64,128]{3,1,0,2:T(8,128)} %copy.33), calls=%async_computation.1 | async-start | bytes 1048576 | tf_op jit(solution)/shard_map/all_to_all | solution.py:71
  64.5 0.1 broadcast_add_fusion
  64.6 9.6 %all-to-all-done = f32[2,8,64,128]{3,1,0,2:T(8,128)S(1)} async-done(((f32[2,8,64,128]{3,1,0,2:T(8,128)}), f32[2,8,64,128]{3,1,0,2:T(8,128)S(1)}, u32[]{:S(2)}, u32[]{:S(2)}) %all-to-all-start) | async-done | bytes 524320 | tf_op jit(solution)/shard_map/all_to_all | solution.py:71
  74.3 0.5 fusion.24
  74.8 0.5 fusion.23
  75.3 0.5 fusion.9
  75.8 0.5 fusion.56
  76.3 0.5 fusion.10
  76.9 0.5 fusion.59
  77.4 0.5 fusion.7
  77.9 0.5 fusion.8
  78.5 0.3 copy.35
  78.8 12.1 %all_to_all.30 = f32[2,64,8,128]{3,2,0,1:T(8,128)S(1)} all-to-all(f32[2,64,8,128]{3,2,0,1:T(8,128)S(1)} %copy.35), channel_id=1, replica_groups=mesh['grid'=8,'band'=4] {'grid'}, dimensions={1} | all-to-all | bytes 1048576 | tf_op jit(solution)/shard_map/all_to_all | solution.py:76
  91.0 0.5 fusion.16
  91.5 0.5 fusion.20
  92.1 0.5 fusion.5
  92.6 0.5 fusion.6
  93.1 0.6 fusion.37
  93.8 0.6 fusion.4
  94.4 0.0 copy-start
  94.4 0.0 copy-start.2
  94.4 0.1 slice_add_fusion
  94.5 0.0 copy-start.1
  94.5 0.4 copy.68
  94.9 0.9 copy-done
  95.8 0.0 copy-done.2
  95.8 1.8 %fusion.3 = bf16[8,8,64,128]{3,0,2,1:T(8,128)(2,1)S(1)} fusion(f32[8,64,128,2]{2,3,1,0:T(2,128)S(1)} %bitcast.140, bf16[8,8,64,128]{3,2,1,0:T(8,128)(2,1)S(1)} %copy-done, s32[8]{0:T(128)S(1)} %copy-done.2), kind=kOutput, calls=%fused_computation.4 | convolution fusion | flops 14155792 | bytes 2621472 | tf_op jit(solution)/shard_map/dot_general | solution.py:108
  97.6 0.0 copy-done.1
  97.6 1.2 %copy.39 = bf16[8,8,64,128]{3,2,1,0:T(8,128)(2,1)} copy(bf16[8,8,64,128]{3,0,2,1:T(8,128)(2,1)S(1)} %fusion.3) | data formatting | bytes 2097152
  (9 shorter events, 0.2 us)
Async XLA Ops:
  7.2 30.0 %reduce-scatter.2.cloned.1.call-start = ((), (), s32[]{:S(2)}) async-start(), calls=%async_computation.3 | async-start | bytes 655360 | tf_op jit(solution)/shard_map/reduce_scatter | solution.py:97
  60.9 13.3 %all-to-all-start = ((f32[2,8,64,128]{3,1,0,2:T(8,128)}), f32[2,8,64,128]{3,1,0,2:T(8,128)S(1)}, u32[]{:S(2)}, u32[]{:S(2)}) async-start(f32[2,8,64,128]{3,1,0,2:T(8,128)} %copy.33), calls=%async_computation.1 | async-start | bytes 1048576 | tf_op jit(solution)/shard_map/all_to_all | solution.py:71
  94.4 1.4 %copy-start = (bf16[8,8,64,128]{3,2,1,0:T(8,128)(2,1)S(1)}, bf16[8,8,64,128]{3,2,1,0:T(8,128)(2,1)}, u32[]{:S(2)}) copy-start(bf16[8,8,64,128]{3,2,1,0:T(8,128)(2,1)} %param.4) | copy-start | bytes 3145732
  94.4 1.4 %copy-start.2 = (s32[8]{0:T(128)S(1)}, s32[8]{0:T(128)}, u32[]{:S(2)}) copy-start(s32[8]{0:T(128)} %param.6) | copy-start | bytes 100
  94.5 3.2 %copy-start.1 = (f32[2,8,64,128]{3,2,1,0:T(8,128)}, f32[2,8,64,128]{3,2,1,0:T(8,128)S(1)}, u32[]{:S(2)}) copy-start(f32[2,8,64,128]{3,2,1,0:T(8,128)S(1)} %slice_add_fusion) | copy-start | bytes 1572868
Sparse Core Ops, SparseCore 0:
  12.6 24.5 reduce-scatter.1
where the time goes:
time: 106 us
  waiting for transfers between devices  34.3 us (32%)
  blocking collectives  29.4 us (28%)
  matrix products  16 us (15%)
  between operations  14.3 us (13%)
  local copies, waits for them, and re-layouts  5.2 us (5%)
  starting transfers between devices  3.67 us (3%)
  other arithmetic  2.81 us (3%)
    reduce_scatter x1, waiting for transfers between devices, local(): lax.psum_scatter(partial_value, 'band', scatter_dimension=2, tiled=True)  24.7 us
    all_gather x1, blocking collectives, local(): whole = lax.all_gather(fields, 'band', axis=2, tiled=True)  17.2 us
    all_to_all x1, blocking collectives, solve_hartree(): lax.all_to_all(back, 'grid', split_axis=1, concat_axis=2, tiled=True)  12.1 us
    all_to_all x1, waiting for transfers between devices, solve_hartree(): lax.all_to_all(jnp.stack([real_y, imag_y]), 'grid', split_axis=2, concat_...  9.6 us
    dot_general x16, matrix products, along(): return jnp.einsum(form, table, field, precision=highest)  8.32 us
    all_to_all x1, starting transfers between devices, solve_hartree(): lax.all_to_all(jnp.stack([real_y, imag_y]), 'grid', split_axis=2, concat_...  3.63 us
    dot_general x1, matrix products, local(): jnp.dot(weights, squares, precision=highest).reshape(2, planes, rows, cols)  3.45 us
    unnamed x8, local copies, waits for them, and re-layouts  2.57 us
  transfers between devices with their start and end apart: 2, of which 2 were waited for; matrix products, arithmetic and copies ran while one was open for 0% of the time, Pallas kernels for 0%

commit v1 on v0

--- a/solution.py
+++ b/solution.py
@@ -7,6 +7,12 @@
 NZ = 64
 spacing = 0.25
 highest = lax.Precision.HIGHEST
+
+
+def swap_blocks(value, name, split, join):
+    shards = jnp.split(value, lax.axis_size(name), axis=split)
+    arrived = lax.all_to_all(jnp.stack(shards), name, 0, 0)
+    return jnp.concatenate(arrived, axis=join)
 
 
 def tables(count):
@@ -68,9 +74,7 @@
     real_x = jnp.dot(net, cos_x, precision=highest)
     imag_x = -jnp.dot(net, sin_x, precision=highest)
     real_y, imag_y = forward_y(cos_y, sin_y, real_x, imag_x)
-    moved = lax.all_to_all(
-        jnp.stack([real_y, imag_y]), "grid", split_axis=2, concat_axis=1, tiled=True
-    )
+    moved = swap_blocks(jnp.stack([real_y, imag_y]), "grid", 2, 1)
     kernel = kernel_at(depth, row_index, rows, jnp.arange(cols, dtype=jnp.int32), cols)
     back = z_kernel(cos_z, sin_z, moved, kernel)
     returned = lax.all_to_all(back, "grid", split_axis=1, concat_axis=2, tiled=True)

time: 106 us -> 110 us (1.038)
  other arithmetic: 2.81 us -> 7.87 us
  local copies, waits for them, and re-layouts: 5.2 us -> 4.1 us
    unnamed x0 -> x7, other arithmetic: none -> 4.47 us
    another operation x1 -> x0, local copies, waits for them, and re-layouts: 1.1 us -> none  [solve_hartree(): jnp.stack([real_y, imag_y])]
where the time goes in v1:
time: 110 us
  waiting for transfers between devices  34.3 us (31%)
  blocking collectives  29.4 us (27%)
  matrix products  16.1 us (15%)
  between operations  14.3 us (13%)
  other arithmetic  7.87 us (7%)
  local copies, waits for them, and re-layouts  4.1 us (4%)
  starting transfers between devices  3.67 us (3%)
    reduce_scatter x1, waiting for transfers between devices, local(): lax.psum_scatter(partial_value, 'band', scatter_dimension=2, tiled=True)  24.7 us
    all_gather x1, blocking collectives, local(): whole = lax.all_gather(fields, 'band', axis=2, tiled=True)  17.2 us
    all_to_all x1, blocking collectives, solve_hartree(): lax.all_to_all(back, 'grid', split_axis=1, concat_axis=2, tiled=True)  12.1 us
    all_to_all x1, waiting for transfers between devices, swap_blocks(): arrived = lax.all_to_all(jnp.stack(shards), name, 0, 0)  9.6 us
    dot_general x16, matrix products, along(): return jnp.einsum(form, table, field, precision=highest)  8.37 us
    unnamed x7, other arithmetic  4.47 us
    all_to_all x1, starting transfers between devices, swap_blocks(): arrived = lax.all_to_all(jnp.stack(shards), name, 0, 0)  3.63 us
    dot_general x1, matrix products, local(): jnp.dot(weights, squares, precision=highest).reshape(2, planes, rows, cols)  3.45 us
  transfers between devices with their start and end apart: 2, of which 2 were waited for; matrix products, arithmetic and copies ran while one was open for 0% of the time, Pallas kernels for 0%

profile of v1, /device:TPU:0, one launch (start us, length us, event | category | flops | bytes accessed | tf_op | source)
XLA Modules:
  0.0 109.7 jit_solution(12752279769898726653)
XLA Ops:
  7.2 0.0 reduce-scatter.2.cloned.1.call-start
  7.2 0.7 convert_element_type.76
  7.9 3.5 %fusion.1 = f32[2,8,64,128]{3,0,2,1:T(2,128)S(1)} fusion(bf16[8,8,64,128]{3,2,1,0:T(8,128)(2,1)} %param.4, f32[8]{0:T(128)S(1)} %convert_element_type.76, s32[8]{0:T(128)} %param.6), kind=kOutput, calls=%fused_computation.3 | convolution fusion | flops 13631536 | bytes 1572928 | tf_op jit(solution)/shard_map/dot_general | solution.py:100
  11.3 1.1 %copy.35 = f32[2,8,64,128]{3,1,0,2:T(8,128)} copy(f32[2,8,64,128]{3,0,2,1:T(2,128)S(1)} %fusion.1) | data formatting | bytes 1048576 | tf_op jit(solution)/shard_map/dot_general | solution.py:100
  12.4 0.0 reduce-scatter.2.cloned.1.call-update
  12.5 24.7 %reduce-scatter.2.cloned.1.call-done = f32[2,8,16,128]{3,1,0,2:T(8,128)} async-done(((f32[2,8,64,128]{3,1,0,2:T(8,128)}), f32[2,8,16,128]{3,1,0,2:T(8,128)}) %reduce-scatter.2.cloned.1.call-update) | async-done | bytes 131088 | tf_op jit(solution)/shard_map/reduce_scatter | solution.py:101
  37.2 1.0 cbrt_negate_fusion
  38.2 0.9 fusion.61
  39.1 17.2 %all_gather.3 = f32[3,8,64,128]{3,2,1,0:T(8,128)S(1)} all-gather(f32[3,8,16,128]{3,2,1,0:T(8,128)S(1)} %pad_maximum_fusion.1), channel_id=1, replica_groups=mesh['grid'=8,'band'=4] {'band'}, dimensions={2}, use_global_device_ids=true | all-gather | bytes 983040 | tf_op jit(solution)/shard_map/all_gather | solution.py:109
  56.3 0.6 convolution_negate_fusion
  57.0 0.6 fusion.22
  57.6 0.5 fusion.91
  58.1 0.5 fusion.89
  58.6 0.5 fusion.12
  59.2 0.5 fusion.11
  59.7 0.6 fusion.41
  60.3 0.6 fusion.44
  61.0 0.6 fusion.47
  61.6 0.6 fusion.50
  62.3 0.6 fusion.53
  62.9 0.6 fusion.56
  63.5 0.6 fusion.38
  64.2 0.6 fusion.58
  64.8 3.6 %all-to-all-start = ((f32[8,2,8,8,128]{4,3,2,1,0:T(8,128)}), f32[8,2,8,8,128]{4,3,2,1,0:T(8,128)S(1)}, u32[]{:S(2)}, u32[]{:S(2)}) async-start(f32[8,2,8,8,128]{4,3,2,1,0:T(8,128)} %fusion.58), calls=%async_computation.1 | async-start | bytes 1048576 | tf_op jit(solution)/shard_map/all_to_all | solution.py:14
  68.5 0.1 broadcast_add_fusion
  68.6 9.6 %all-to-all-done = f32[8,2,8,8,128]{4,3,2,1,0:T(8,128)S(1)} async-done(((f32[8,2,8,8,128]{4,3,2,1,0:T(8,128)}), f32[8,2,8,8,128]{4,3,2,1,0:T(8,128)S(1)}, u32[]{:S(2)}, u32[]{:S(2)}) %all-to-all-start) | async-done | bytes 524320 | tf_op jit(solution)/shard_map/all_to_all | solution.py:14
  78.2 0.5 fusion.27
  78.7 0.5 fusion.31
  79.3 0.5 fusion.9
  79.8 0.5 fusion.10
  80.4 0.5 fusion.86
  80.9 0.5 fusion.83
  81.4 0.5 fusion.8
  81.9 0.5 fusion.7
  82.5 0.3 copy.43
  82.8 12.1 %all_to_all.20 = f32[2,64,8,128]{3,2,0,1:T(8,128)S(1)} all-to-all(f32[2,64,8,128]{3,2,0,1:T(8,128)S(1)} %copy.43), channel_id=1, replica_groups=mesh['grid'=8,'band'=4] {'grid'}, dimensions={1} | all-to-all | bytes 1048576 | tf_op jit(solution)/shard_map/all_to_all | solution.py:80
  95.0 0.5 fusion.16
  95.5 0.5 fusion.20
  96.1 0.5 fusion.5
  96.6 0.5 fusion.6
  97.1 0.6 fusion.64
  97.8 0.6 fusion.4
  98.4 0.0 copy-start
  98.4 0.0 copy-start.2
  98.4 0.1 slice_add_fusion
  98.5 0.0 copy-start.1
  98.5 0.4 copy.83
  98.9 0.9 copy-done
  99.8 0.0 copy-done.2
  99.8 1.8 %fusion.3 = bf16[8,8,64,128]{3,0,2,1:T(8,128)(2,1)S(1)} fusion(f32[8,64,128,2]{2,3,1,0:T(2,128)S(1)} %bitcast.159, bf16[8,8,64,128]{3,2,1,0:T(8,128)(2,1)S(1)} %copy-done, s32[8]{0:T(128)S(1)} %copy-done.2), kind=kOutput, calls=%fused_computation.4 | convolution fusion | flops 14155792 | bytes 2621472 | tf_op jit(solution)/shard_map/dot_general | solution.py:112
  101.6 0.0 copy-done.1
  101.6 1.2 %copy.47 = bf16[8,8,64,128]{3,2,1,0:T(8,128)(2,1)} copy(bf16[8,8,64,128]{3,0,2,1:T(8,128)(2,1)S(1)} %fusion.3) | data formatting | bytes 2097152
  (8 shorter events, 0.2 us)
Async XLA Ops:
  7.2 30.0 %reduce-scatter.2.cloned.1.call-start = ((), (), s32[]{:S(2)}) async-start(), calls=%async_computation.3 | async-start | bytes 655360 | tf_op jit(solution)/shard_map/reduce_scatter | solution.py:101
  64.8 13.3 %all-to-all-start = ((f32[8,2,8,8,128]{4,3,2,1,0:T(8,128)}), f32[8,2,8,8,128]{4,3,2,1,0:T(8,128)S(1)}, u32[]{:S(2)}, u32[]{:S(2)}) async-start(f32[8,2,8,8,128]{4,3,2,1,0:T(8,128)} %fusion.58), calls=%async_computation.1 | async-start | bytes 1048576 | tf_op jit(solution)/shard_map/all_to_all | solution.py:14
  98.4 1.4 %copy-start = (bf16[8,8,64,128]{3,2,1,0:T(8,128)(2,1)S(1)}, bf16[8,8,64,128]{3,2,1,0:T(8,128)(2,1)}, u32[]{:S(2)}) copy-start(bf16[8,8,64,128]{3,2,1,0:T(8,128)(2,1)} %param.4) | copy-start | bytes 3145732
  98.4 1.4 %copy-start.2 = (s32[8]{0:T(128)S(1)}, s32[8]{0:T(128)}, u32[]{:S(2)}) copy-start(s32[8]{0:T(128)} %param.6) | copy-start | bytes 100
  98.5 3.2 %copy-start.1 = (f32[2,8,64,128]{3,2,1,0:T(8,128)}, f32[2,8,64,128]{3,2,1,0:T(8,128)S(1)}, u32[]{:S(2)}) copy-start(f32[2,8,64,128]{3,2,1,0:T(8,128)S(1)} %slice_add_fusion) | copy-start | bytes 1572868
Sparse Core Ops, SparseCore 0:
  12.6 24.5 reduce-scatter.1
